TPU v7x, 32 devices: a whole 2x2x4 slice. The times are simulated.
32 devices in a mesh: dp: 8 (over z, y), mp: 4 (over x, core).
Axes of the slice: x: 2, y: 2, z: 4, core: 2. Of those that a mesh axis runs over, the one named last changes fastest.
Arguments:
- tokens: bfloat16 [2048, 4096], P('dp', 'mp'), may hold values from -6 to 6
- router_weight: bfloat16 [4096, 64], P('mp'), may hold values from -1 to 1
- valid_count: int32 [8], P('dp'), may hold values from 64 to 256, as said below
- expert_id: int32 [2048], P('dp'), may hold values from 0 to 63, as said below
- slot_id: int32 [2048], P('dp'), may hold values from 0 to 5
Outputs:
- gates: float32 [2048], P('dp')
- dispatched: bfloat16 [384, 8, 4096], P('dp', None, 'mp')
Inputs may be any that keep to these rules, and one draw needn't show every extreme that they name: Group g's live tokens are its first valid_count[g] positions; the last group is full. Within one group no two positions share an expert and a slot. Flat slots expert_id * 6 + slot_id are held 48 in a row by one owner; one group's positions take at most 32 slots of any owner, and in every group some owner has 32 of its slots taken by live tokens.
All inputs are finite; a program needn't handle non-finite values.
Results may differ from a plain program's by a relative error of at most 0.001.
Values may be sent and summed in bfloat16 or wider, within the bound.
A program may use at most 64 MiB of HBM per device.

v0:
```python
import jax
import jax.numpy as jnp
from jax import lax
from jax.sharding import PartitionSpec as P

E = 64
ITERS = 5
CAP = 6


def dispatch(tokens, live, expert_id, slot_id):
    total_slots = E * CAP
    target = expert_id * CAP + slot_id
    placed = jnp.where(live, target, total_slots)
    buffer = (
        jnp.zeros((total_slots, tokens.shape[1]), jnp.bfloat16).at[placed].set(tokens, mode="drop")
    )
    return lax.all_to_all(buffer[:, None, :], "dp", split_axis=0, concat_axis=1, tiled=True)


def balance(logits, live, expert_id, total, column_sum):
    experts = logits.shape[1]
    affinity = jnp.exp(logits)
    weight = live.astype(jnp.float32)
    col_scale = jnp.ones((experts,), jnp.float32)
    row_scale = jnp.ones((logits.shape[0],), jnp.float32)
    for sweep in range(ITERS):
        row_scale = experts / jnp.sum(affinity * col_scale[None, :], axis=1)
        column = column_sum(jnp.sum(affinity * (weight * row_scale)[:, None], axis=0))
        col_scale = total / column
    chosen = expert_id[:, None] == jnp.arange(experts, dtype=jnp.int32)[None, :]
    picked = jnp.sum(jnp.where(chosen, affinity * col_scale[None, :], 0.0), axis=1)
    return weight * row_scale * picked


def local(tokens, router_weight, valid_count, expert_id, slot_id):
    rows = tokens.shape[0]
    live = jnp.arange(rows, dtype=jnp.int32) < valid_count[0]
    dispatched = None
    total = lax.psum(valid_count.astype(jnp.float32)[0], "dp")
    partial_logits = jnp.dot(tokens, router_weight, preferred_element_type=jnp.float32)
    logits = lax.psum(partial_logits, "mp")

    def group_sum(partial_value):
        return lax.psum(partial_value, "dp")

    gates = balance(logits, live, expert_id, total, group_sum)
    dispatched = dispatch(tokens, live, expert_id, slot_id)
    return (gates, dispatched)


def solution(mesh):
    placed = (P("dp", "mp"), P("mp", None), P("dp"), P("dp"), P("dp"))
    return jax.shard_map(
        local, mesh=mesh, in_specs=placed, out_specs=(P("dp"), P("dp", None, "mp")), check_vma=False
    )
```

profile of v0, /device:TPU:0, one launch (start us, length us, event | category | flops | bytes accessed | tf_op | source)
XLA Modules:
  0.0 163.1 jit_solution(8325949597759556054)
XLA Ops:
  7.2 0.0 copy-start
  7.2 0.0 all-reduce.3.cloned.1.call-start
  7.2 0.8 copy-done
  8.1 1.9 %fusion.2 = f32[256,64]{0,1:T(8,128)} fusion(bf16[256,1024]{1,0:T(8,128)(2,1)} %param.5, bf16[1024,64]{0,1:T(8,128)(2,1)S(1)} %copy-done), kind=kOutput, calls=%fused_computation.27 | convolution fusion | flops 33554432 | bytes 720896 | tf_op jit(solution)/shard_map/dot_general | solution.py:41
  10.0 0.0 all-reduce.3.cloned.1.call-update
  10.7 0.7 compare_select_fusion
  11.4 2.4 %scatter_custom_fusion = bf16[384,1024]{1,0:T(8,128)(2,1)S(1)} fusion(s32[256]{0:T(256)S(1)} %compare_select_fusion, bf16[256,1024]{1,0:T(8,128)(2,1)} %param.5, bf16[]{:T(256)} %constant.14.clone.1), kind=kCustom, calls=%fused_computation.1 | custom fusion | bytes 786944 | tf_op jit(solution)/shard_map/scatter | solution.py:16
  13.8 0.5 broadcast.88
  14.3 1.2 reduce
  15.6 0.0 copy-start.1
  15.6 1.5 reshape.53
  17.0 7.3 %all-to-all-start = ((bf16[8,2,24576]{2,1,0:T(2,128)(2,1)}), bf16[8,2,24576]{2,1,0:T(2,128)(2,1)S(1)}, u32[]{:S(2)}, u32[]{:S(2)}) async-start(bf16[8,2,24576]{2,1,0:T(2,128)(2,1)} %reshape.53), calls=%async_computation | async-start | bytes 1572864 | tf_op jit(solution)/shard_map/all_to_all | solution.py:18
  24.3 20.2 %all-reduce.3.cloned.1.call-done = f32[256,64]{0,1:T(8,128)} async-done(((f32[256,64]{0,1:T(8,128)}), f32[256,64]{0,1:T(8,128)}) %all-reduce.3.cloned.1.call-update) | async-done | bytes 65552 | tf_op jit(solution)/shard_map/psum | solution.py:42
  44.6 0.9 exponential_reduce_fusion
  45.4 1.0 multiply_reduce_fusion.8
  46.4 22.5 %all-reduce = (f32[64]{0:T(128)S(1)}, f32[]{:T(128)}) all-reduce(f32[64]{0:T(128)S(1)} %multiply_reduce_fusion.8, f32[]{:T(128)} %bitcast.1), channel_id=1, replica_groups=mesh['dp'=8,'mp'=4] {'dp'}, use_global_device_ids=true, to_apply=%region_4.0 | all-reduce | flops 65 | bytes 520 | tf_op jit(solution)/shard_map/psum | solution.py:45
  68.9 0.6 broadcast_divide_fusion.4
  69.6 0.9 multiply_reduce_fusion.7
  70.5 1.0 multiply_reduce_fusion.6
  71.5 17.1 %psum.52 = f32[64]{0:T(128)S(1)} all-reduce(f32[64]{0:T(128)S(1)} %multiply_reduce_fusion.6), channel_id=1, replica_groups=mesh['dp'=8,'mp'=4] {'dp'}, use_global_device_ids=true, to_apply=%region_7.0 | all-reduce | flops 64 | bytes 512 | tf_op jit(solution)/shard_map/psum | solution.py:45
  88.6 0.6 broadcast_divide_fusion.3
  89.3 0.9 multiply_reduce_fusion.5
  90.2 1.0 multiply_reduce_fusion.4
  91.2 19.1 %psum.53 = f32[64]{0:T(128)S(1)} all-reduce(f32[64]{0:T(128)S(1)} %multiply_reduce_fusion.4), channel_id=1, replica_groups=mesh['dp'=8,'mp'=4] {'dp'}, use_global_device_ids=true, to_apply=%region_10.0 | all-reduce | flops 64 | bytes 512 | tf_op jit(solution)/shard_map/psum | solution.py:45
  110.3 0.6 broadcast_divide_fusion.2
  111.0 0.9 multiply_reduce_fusion.3
  111.9 1.0 multiply_reduce_fusion.2
  112.9 17.1 %psum.54 = f32[64]{0:T(128)S(1)} all-reduce(f32[64]{0:T(128)S(1)} %multiply_reduce_fusion.2), channel_id=1, replica_groups=mesh['dp'=8,'mp'=4] {'dp'}, use_global_device_ids=true, to_apply=%region_13.0 | all-reduce | flops 64 | bytes 512 | tf_op jit(solution)/shard_map/psum | solution.py:45
  130.0 0.6 broadcast_divide_fusion.1
  130.7 0.9 multiply_reduce_fusion.1
  131.6 1.0 multiply_reduce_fusion
  132.6 19.1 %psum.55 = f32[64]{0:T(128)S(1)} all-reduce(f32[64]{0:T(128)S(1)} %multiply_reduce_fusion), channel_id=1, replica_groups=mesh['dp'=8,'mp'=4] {'dp'}, use_global_device_ids=true, to_apply=%region_16.0 | all-reduce | flops 64 | bytes 512 | tf_op jit(solution)/shard_map/psum | solution.py:45
  151.7 0.6 broadcast_divide_fusion
  152.4 0.0 copy-done.1
  152.4 0.9 select_reduce_fusion
  153.3 0.6 fusion.5
  153.9 0.0 all-to-all-done
  153.9 0.8 reshape.54
  154.7 0.3 copy.10
  155.0 1.3 copy.9
  (5 shorter events, 0.0 us)
Async XLA Ops:
  7.2 0.9 copy-start
  7.2 37.4 %all-reduce.3.cloned.1.call-start = ((), (), s32[]{:S(2)}) async-start(), calls=%async_computation.1 | async-start | bytes 131072 | tf_op jit(solution)/shard_map/psum | solution.py:42
  15.6 136.8 %copy-start.1 = (s32[256]{0:T(256)S(1)}, s32[256]{0:T(256)}, u32[]{:S(2)}) copy-start(s32[256]{0:T(256)} %param.8) | copy-start | bytes 3076
  17.0 136.9 %all-to-all-start = ((bf16[8,2,24576]{2,1,0:T(2,128)(2,1)}), bf16[8,2,24576]{2,1,0:T(2,128)(2,1)S(1)}, u32[]{:S(2)}, u32[]{:S(2)}) async-start(bf16[8,2,24576]{2,1,0:T(2,128)(2,1)} %reshape.53), calls=%async_computation | async-start | bytes 1572864 | tf_op jit(solution)/shard_map/all_to_all | solution.py:18
Sparse Core Ops, SparseCore 0:
  10.3 34.2 all-reduce.2
where the time goes:
time: 164 us; the launch traced here: 163 us
  blocking collectives  95 us (58%)
  waiting for transfers between devices  20.3 us (12%)
  other arithmetic  16.1 us (10%)
  between operations  14.8 us (9%)
  local copies, waits for them, and re-layouts  7.63 us (5%)
  starting transfers between devices  7.35 us (4%)
  matrix products  1.95 us (1%)
    psum x5, blocking collectives, group_sum(): return lax.psum(partial_value, 'dp')  95 us
    psum x1, waiting for transfers between devices, local(): logits = lax.psum(partial_logits, 'mp')  20.2 us
    all_to_all x1, starting transfers between devices, dispatch(): lax.all_to_all(buffer[:, None, :], 'dp', split_axis=0, concat_axis=1, til...  7.31 us
    reduce_sum x5, other arithmetic, balance(): jnp.sum(affinity * (weight * row_scale)[:, None], axis=0)  4.8 us
    unnamed x8, local copies, waits for them, and re-layouts  4.71 us
    reduce_sum x5, other arithmetic, balance(): row_scale = experts / jnp.sum(affinity * col_scale[None, :], axis=1)  4.61 us
  transfers between devices with their start and end apart: 2, of which 1 were waited for; matrix products, arithmetic and copies ran while one was open for 13% of the time, Pallas kernels for 0%

commit v1 on v0

--- a/solution.py
+++ b/solution.py
@@ -6,6 +6,11 @@
 E = 64
 ITERS = 5
 CAP = 6
+
+
+def add_all(array, name):
+    shards = lax.all_gather(array, name)
+    return jnp.sum(shards, axis=0)
 
 
 def dispatch(tokens, live, expert_id, slot_id):
@@ -39,7 +44,7 @@
     dispatched = None
     total = lax.psum(valid_count.astype(jnp.float32)[0], "dp")
     partial_logits = jnp.dot(tokens, router_weight, preferred_element_type=jnp.float32)
-    logits = lax.psum(partial_logits, "mp")
+    logits = add_all(partial_logits, "mp")
 
     def group_sum(partial_value):
         return lax.psum(partial_value, "dp")

time: 164 us -> 125 us (0.76)
  waiting for transfers between devices: 20.3 us -> 0.01 us
  between operations: 14.8 us -> 1.46 us
  other arithmetic: 16.1 us -> 7.03 us
  blocking collectives: 95 us -> 101 us
  matrix products: 1.95 us -> 0.28 us
    psum x1 -> x0, waiting for transfers between devices: 20.2 us -> none  [local(): logits = lax.psum(partial_logits, 'mp')]
    all_gather x0 -> x1, blocking collectives: none -> 5.78 us  [add_all(): shards = lax.all_gather(array, name)]
    reduce_sum x5, other arithmetic: 4.8 us -> 0.58 us  [balance(): jnp.sum(affinity * (weight * row_scale)[:, None], axis=0)]
    reduce_sum x5, other arithmetic: 4.61 us -> 0.41 us  [balance(): row_scale = experts / jnp.sum(affinity * col_scale[None, :], axis=1)]
    dot_general x1, matrix products: 1.95 us -> 0.28 us  [local(): jnp.dot(tokens, router_weight, preferred_element_type=jnp.float32)]
    unnamed x8 -> x10, local copies, waits for them, and re-layouts: 4.71 us -> 3.87 us
  transfers between devices with their start and end apart: 2 -> 1, of which waited for: 1 -> 0; matrix products, arithmetic and copies ran while one was open for 13% -> 4% of each run, Pallas kernels for 0% -> 0%
where the time goes in v1:
time: 125 us; the launch traced here: 124 us
  blocking collectives  101 us (81%)
  starting transfers between devices  7.31 us (6%)
  other arithmetic  7.03 us (6%)
  local copies, waits for them, and re-layouts  6.91 us (6%)
  between operations  1.46 us (1%)
    psum x5, blocking collectives, group_sum(): return lax.psum(partial_value, 'dp')  95.6 us
    all_to_all x1, starting transfers between devices, dispatch(): lax.all_to_all(buffer[:, None, :], 'dp', split_axis=0, concat_axis=1, til...  7.31 us
    all_gather x1, blocking collectives, add_all(): shards = lax.all_gather(array, name)  5.78 us
    unnamed x10, local copies, waits for them, and re-layouts  3.87 us
    div x5, other arithmetic, balance(): col_scale = total / column  3.24 us
  transfers between devices with their start and end apart: 1, of which 0 were waited for; matrix products, arithmetic and copies ran while one was open for 4% of the time, Pallas kernels for 0%

profile of v1, /device:TPU:0, one launch (start us, length us, event | category | flops | bytes accessed | tf_op | source)
XLA Modules:
  0.0 124.4 jit_solution(14911172709928967846)
XLA Ops:
  0.6 0.0 copy-start
  1.3 0.7 compare_select_fusion
  2.0 2.4 %scatter_custom_fusion = bf16[384,1024]{1,0:T(8,128)(2,1)S(1)} fusion(s32[256]{0:T(256)S(1)} %compare_select_fusion, bf16[256,1024]{1,0:T(8,128)(2,1)} %param.5, bf16[]{:T(256)} %constant.14.clone.1), kind=kCustom, calls=%fused_computation.1 | custom fusion | bytes 786944 | tf_op jit(solution)/shard_map/scatter | solution.py:21
  4.4 0.5 broadcast.88
  5.0 1.2 reduce
  6.2 0.0 copy-start.1
  6.2 1.5 %reshape.54 = bf16[8,2,24576]{2,1,0:T(2,128)(2,1)} reshape(bf16[384,1024]{1,0:T(8,128)(2,1)S(1)} %reduce) | data formatting | bytes 1572864
  7.7 7.3 %all-to-all-start = ((bf16[8,2,24576]{2,1,0:T(2,128)(2,1)}), bf16[8,2,24576]{2,1,0:T(2,128)(2,1)S(1)}, u32[]{:S(2)}, u32[]{:S(2)}) async-start(bf16[8,2,24576]{2,1,0:T(2,128)(2,1)} %reshape.54), calls=%async_computation | async-start | bytes 1572864 | tf_op jit(solution)/shard_map/all_to_all | solution.py:23
  15.0 0.0 copy-start.2
  15.0 0.0 copy-done
  15.0 0.0 copy-done.1
  15.0 0.3 fusion.2
  15.3 5.8 %all-gather = f32[1024,64]{0,1:T(8,128)S(1)} all-gather(f32[256,64]{0,1:T(8,128)S(1)} %fusion.2), channel_id=2, replica_groups=mesh['dp'=8,'mp'=4] {'mp'}, dimensions={0}, use_global_device_ids=true | all-gather | bytes 327680 | tf_op jit(solution)/shard_map/all_gather | solution.py:12
  21.1 0.1 reshape.50
  21.2 0.2 reduce_sum.108
  21.4 0.1 multiply_reduce_fusion.8
  21.5 23.1 %all-reduce = (f32[64]{0:T(128)S(1)}, f32[]{:T(128)}) all-reduce(f32[64]{0:T(128)S(1)} %multiply_reduce_fusion.8, f32[]{:T(128)} %bitcast.1), channel_id=1, replica_groups=mesh['dp'=8,'mp'=4] {'dp'}, use_global_device_ids=true, to_apply=%region_4.0 | all-reduce | flops 65 | bytes 520 | tf_op jit(solution)/shard_map/psum | solution.py:50
  44.6 0.6 broadcast_divide_fusion.4
  45.3 0.1 multiply_reduce_fusion.7
  45.4 0.1 multiply_reduce_fusion.6
  45.5 18.8 %psum.44 = f32[64]{0:T(128)S(1)} all-reduce(f32[64]{0:T(128)S(1)} %multiply_reduce_fusion.6), channel_id=1, replica_groups=mesh['dp'=8,'mp'=4] {'dp'}, use_global_device_ids=true, to_apply=%region_7.0 | all-reduce | flops 64 | bytes 512 | tf_op jit(solution)/shard_map/psum | solution.py:50
  64.3 0.6 broadcast_divide_fusion.3
  65.0 0.1 multiply_reduce_fusion.5
  65.1 0.1 multiply_reduce_fusion.4
  65.2 17.4 %psum.45 = f32[64]{0:T(128)S(1)} all-reduce(f32[64]{0:T(128)S(1)} %multiply_reduce_fusion.4), channel_id=1, replica_groups=mesh['dp'=8,'mp'=4] {'dp'}, use_global_device_ids=true, to_apply=%region_10.0 | all-reduce | flops 64 | bytes 512 | tf_op jit(solution)/shard_map/psum | solution.py:50
  82.6 0.6 broadcast_divide_fusion.2
  83.3 0.1 multiply_reduce_fusion.3
  83.4 0.1 multiply_reduce_fusion.2
  83.5 18.8 %psum.46 = f32[64]{0:T(128)S(1)} all-reduce(f32[64]{0:T(128)S(1)} %multiply_reduce_fusion.2), channel_id=1, replica_groups=mesh['dp'=8,'mp'=4] {'dp'}, use_global_device_ids=true, to_apply=%region_13.0 | all-reduce | flops 64 | bytes 512 | tf_op jit(solution)/shard_map/psum | solution.py:50
  102.3 0.6 broadcast_divide_fusion.1
  103.0 0.1 multiply_reduce_fusion.1
  103.1 0.1 multiply_reduce_fusion
  103.2 17.4 %psum.47 = f32[64]{0:T(128)S(1)} all-reduce(f32[64]{0:T(128)S(1)} %multiply_reduce_fusion), channel_id=1, replica_groups=mesh['dp'=8,'mp'=4] {'dp'}, use_global_device_ids=true, to_apply=%region_16.0 | all-reduce | flops 64 | bytes 512 | tf_op jit(solution)/shard_map/psum | solution.py:50
  120.7 0.6 broadcast_divide_fusion
  121.3 0.0 copy-done.2
  121.3 0.1 select_reduce_fusion
  121.4 0.6 fusion.5
  122.0 0.0 all-to-all-done
  122.0 0.8 reshape.55
  122.8 0.3 copy.10
  123.1 1.3 %copy.9 = bf16[48,8,1024]{2,1,0:T(8,128)(2,1)} copy(bf16[48,8,1024]{2,0,1:T(8,128)(2,1)S(1)} %bitcast.21) | data formatting | bytes 1572864
  (6 shorter events, 0.1 us)
Async XLA Ops:
  0.6 14.3 %copy-start = (bf16[1024,64]{0,1:T(8,128)(2,1)S(1)}, bf16[1024,64]{0,1:T(8,128)(2,1)}, u32[]{:S(2)}) copy-start(bf16[1024,64]{0,1:T(8,128)(2,1)} %param.6) | copy-start | bytes 393220
  6.2 8.8 %copy-start.1 = (bf16[256,1024]{1,0:T(8,128)(2,1)S(1)}, bf16[256,1024]{1,0:T(8,128)(2,1)}, u32[]{:S(2)}) copy-start(bf16[256,1024]{1,0:T(8,128)(2,1)} %param.5) | copy-start | bytes 1572868
  7.7 114.4 %all-to-all-start = ((bf16[8,2,24576]{2,1,0:T(2,128)(2,1)}), bf16[8,2,24576]{2,1,0:T(2,128)(2,1)S(1)}, u32[]{:S(2)}, u32[]{:S(2)}) async-start(bf16[8,2,24576]{2,1,0:T(2,128)(2,1)} %reshape.54), calls=%async_computation | async-start | bytes 1572864 | tf_op jit(solution)/shard_map/all_to_all | solution.py:23
  15.0 106.4 %copy-start.2 = (s32[256]{0:T(256)S(1)}, s32[256]{0:T(256)}, u32[]{:S(2)}) copy-start(s32[256]{0:T(256)} %param.8) | copy-start | bytes 3076
